TPU v7x, 32 devices: a whole 2x2x4 slice. The times are simulated.
32 devices in a mesh: rows: 32 (over z, y, x, core).
Axes of the slice: x: 2, y: 2, z: 4, core: 2. Of those that a mesh axis runs over, the one named last changes fastest.
Arguments:
- blocks: float32 [512, 4, 256, 256], P('rows'), may hold values from -0.125 to 0.125
- block_cols: int32 [512, 4], P('rows'), may hold values from 0 to 511, as said below
- live_counts: int32 [512], P('rows'), may hold values from 1 to 4, as said below
- onsite_energy: float32 [131072], P('rows'), may hold values from -2 to 2
- precond: float32 [512, 256, 256], P('rows')
- vectors: float32 [32, 131072], P(None, 'rows'), may hold values from -6 to 6
- prev_vectors: float32 [32, 131072], P(None, 'rows'), may hold values from -6 to 6
- prev_image: float32 [32, 131072], P(None, 'rows'), may hold values from -6 to 6
Outputs:
- correction: float32 [32, 131072], P(None, 'rows')
- reduced: float32 [96, 96], replicated
Inputs may be any that keep to these rules, and one draw needn't show every extreme that they name: block_cols[b, s] = (b + o) mod 512, with the offsets o of one block-row distinct and within 0 to 4; every slot holds a valid block-column. Slots s < live_counts[b] are live, the rest are ignored; some block-row has 4 live slots in every draw.
All inputs are finite; a program needn't handle non-finite values.
Results may differ from a plain program's by a relative error of at most 0.00026.
Values sent between devices are 32-bit elements; how exact they have to be, the bound alone decides.
A program may use at most 128 MiB of HBM per device.

v0:
```python
import jax
import jax.numpy as jnp
from jax import lax
from jax.sharding import PartitionSpec as P

HB = 4
ITERS = 3


def shifted(block, axis, distance):
    devices = range(lax.axis_size(axis))
    route = [((i - distance) % len(devices), i) for i in devices]
    return lax.ppermute(block, axis, route)


def padded_apply(source, tiles, offsets, counts_here, extended, extent):
    slot_count = tiles.shape[1]
    live_mask = (
        lax.broadcasted_iota(jnp.int32, (tiles.shape[0], slot_count), 1) < counts_here[:, None]
    ).astype(jnp.float32)
    one_hot = (offsets[:, :, None] == lax.broadcasted_iota(jnp.int32, (1, 1, extent), 2)).astype(
        jnp.float32
    ) * live_mask[:, :, None]
    moved = jnp.einsum("kbi,bsij->kbsj", source, tiles, precision=lax.Precision.HIGHEST)
    spread = jnp.einsum("bse,kbsj->kej", one_hot, moved, precision=lax.Precision.HIGHEST)
    forward_part = None
    picked = jnp.einsum("bse,kej->kbsj", one_hot, extended, precision=lax.Precision.HIGHEST)
    forward_part = jnp.einsum("bsij,kbsj->kbi", tiles, picked, precision=lax.Precision.HIGHEST)
    return (forward_part, spread)


def apply_tiles(source, tiles, offsets, counts_here, extended, extent):
    return padded_apply(source, tiles, offsets, counts_here, extended, extent)


def local(
    blocks, block_cols, live_counts, onsite_energy, precond, vectors, prev_vectors, prev_image
):
    block_rows = blocks.shape[0]
    block_size = blocks.shape[2]
    vec_count = vectors.shape[0]
    local_rows = block_rows * block_size
    reach = HB
    total_blocks = block_rows * lax.axis_size("rows")
    first_block = lax.axis_index("rows") * block_rows
    own_offsets = (block_cols - first_block) % total_blocks

    def operate(field):
        source = field.reshape(vec_count, block_rows, block_size)
        right_rows = shifted(field[:, : reach * block_size], "rows", -1)
        extended = jnp.concatenate([field, right_rows], axis=1).reshape(
            vec_count, block_rows + reach, block_size
        )
        forward_part, spread = apply_tiles(
            source, blocks, own_offsets, live_counts, extended, block_rows + reach
        )
        outgoing = spread[:, block_rows:].reshape(vec_count, reach * block_size)
        incoming = shifted(outgoing, "rows", 1)
        own_part = spread[:, :block_rows].reshape(vec_count, local_rows)
        own_part = own_part + jnp.pad(incoming, ((0, 0), (0, local_rows - reach * block_size)))
        return (
            onsite_energy[None, :] * field + forward_part.reshape(vec_count, local_rows) + own_part
        )

    image = operate(vectors)
    numerator_part = jnp.sum(vectors * image, axis=1)
    denominator_part = jnp.sum(vectors * vectors, axis=1)
    numerator, denominator = lax.psum((numerator_part, denominator_part), "rows")
    quotient = numerator / denominator
    remainder = -(image - quotient[:, None] * vectors)
    correction = jnp.zeros_like(vectors)
    hcorr = jnp.zeros_like(vectors)
    for iteration in range(ITERS):
        shaped = remainder.reshape(vec_count, block_rows, block_size)
        search = jnp.einsum(
            "bij,kbj->kbi", precond, shaped, precision=lax.Precision.HIGHEST
        ).reshape(vec_count, local_rows)
        applied = operate(search) - quotient[:, None] * search
        cross_sum, self_sum = lax.psum(
            (jnp.sum(applied * remainder, axis=1), jnp.sum(applied * applied, axis=1)), "rows"
        )
        step_size = cross_sum / (self_sum + 1.0)
        correction = correction + step_size[:, None] * search
        hcorr = hcorr + step_size[:, None] * (applied + quotient[:, None] * search)
        remainder = remainder - step_size[:, None] * applied
    basis = jnp.concatenate([vectors, prev_vectors, correction], axis=0)
    himage = jnp.concatenate([image, prev_image, hcorr], axis=0)
    gram_matrix, projected = lax.psum(
        (
            jnp.dot(basis, basis.T, precision=lax.Precision.HIGHEST),
            jnp.dot(basis, himage.T, precision=lax.Precision.HIGHEST),
        ),
        "rows",
    )
    gram_matrix = gram_matrix + jnp.eye(gram_matrix.shape[0], dtype=jnp.float32)
    factor = jnp.linalg.cholesky(gram_matrix)
    half_way = jax.scipy.linalg.solve_triangular(factor, projected, lower=True)
    reduced = jax.scipy.linalg.solve_triangular(factor, half_way.T, lower=True).T
    return (correction, reduced)


def solution(mesh):
    placed = (
        P("rows", None, None, None),
        P("rows", None),
        P("rows"),
        P("rows"),
        P("rows", None, None),
        P(None, "rows"),
        P(None, "rows"),
        P(None, "rows"),
    )
    return jax.shard_map(
        local, mesh=mesh, in_specs=placed, out_specs=(P(None, "rows"), P()), check_vma=False
    )
```

profile of v0, /device:TPU:0, one launch (start us, length us, event | category | flops | bytes accessed | tf_op | source)
XLA Modules:
  0.0 523.8 jit_solution(8646611388129024031)
XLA Ops:
  8.1 6.5 %collective-permute-start = (f32[32,1024]{1,0:T(8,128)S(1)}, f32[32,1024]{1,0:T(8,128)S(1)}, u32[]{:S(2)}, u32[]{:S(2)}) collective-permute-start(f32[32,1024]{1,0:T(8,128)S(1)} %slice.46), channel_id=1, source_target_pairs={{1,0},{2,1},{3,2},{4,3},{5,4},{6,5},{7,6},{8,7},{9,8},{10,9},{11,1... | collective-permute-start | bytes 393224 | tf_op jit(solution)/shard_map/ppermute | solution.py:13
  17.2 13.9 %fusion.78 = f32[16,4,256,32]{2,3,1,0:T(8,128)S(1)} fusion(f32[16,4,256,256]{3,2,1,0:T(8,128)} %param.10, f32[32,16,256,1]{2,1,0,3:T(8,128)S(1)} %bitcast.225), kind=kOutput, calls=%fused_computation.69 | convolution fusion | flops 1610612736 | bytes 19398656 | tf_op jit(solution)/shard_map/kbi,bsij->kbsj/dot_general | solution.py:24
  31.0 2.4 fusion.30
  36.5 18.8 %fusion.42 = f32[16,4,8,256]{3,2,1,0:T(8,128)S(1)} fusion(f32[16,4,256,256]{3,2,1,0:T(8,128)} %param.10, f32[32,256,16,4]{1,2,3,0:T(8,128)S(1)} %fusion.61), kind=kOutput, calls=%fused_computation.35 | convolution fusion | flops 1610612736 | bytes 19398656 | tf_op jit(solution)/shard_map/bsij,kbsj->kbi/dot_general | solution.py:28
  55.7 38.3 %all-reduce.8 = (f32[32]{0:T(128)S(1)}, f32[32]{0:T(128)S(1)}) all-reduce(f32[32]{0:T(128)S(1)} %get-tuple-element.14, f32[32]{0:T(128)S(1)} %get-tuple-element.13), channel_id=1, replica_groups=mesh['rows'=32] {'rows'}, use_global_device_ids=true, to_apply=%region_1.2 | all-reduce | flops 64 | bytes 512 | tf_op jit(solution)/shard_map/psum | solution.py:68
  94.1 6.1 %fusion.69 = f32[16,32,256]{2,1,0:T(8,128)S(1)} fusion(f32[16,256,256]{2,1,0:T(8,128)} %param.14, f32[4,16,8,256]{3,2,1,0:T(8,128)S(1)} %bitcast.220), kind=kOutput, calls=%fused_computation.60 | convolution fusion | flops 402653184 | bytes 5242880 | tf_op jit(solution)/shard_map/bij,kbj->kbi/dot_general | solution.py:75
  100.2 13.0 %fusion.76 = f32[16,32,4,256]{3,1,2,0:T(8,128)S(1)} fusion(f32[16,4,256,256]{3,2,1,0:T(8,128)} %param.10, f32[16,32,256]{2,1,0:T(8,128)S(1)} %fusion.69), kind=kOutput, calls=%fused_computation.67 | convolution fusion | flops 1610612736 | bytes 19398656 | tf_op jit(solution)/shard_map/kbi,bsij->kbsj/dot_general | solution.py:24
  115.2 2.4 fusion.33
  121.2 18.8 %fusion.45 = f32[16,4,8,256]{3,2,1,0:T(8,128)S(1)} fusion(f32[16,4,256,256]{3,2,1,0:T(8,128)} %param.10, f32[32,256,16,4]{1,2,3,0:T(8,128)S(1)} %fusion.59), kind=kOutput, calls=%fused_computation.36 | convolution fusion | flops 1610612736 | bytes 19398656 | tf_op jit(solution)/shard_map/bsij,kbsj->kbi/dot_general | solution.py:28
  141.9 41.1 %all-reduce.7 = (f32[32]{0:T(128)S(1)}, f32[32]{0:T(128)S(1)}) all-reduce(f32[32]{0:T(128)S(1)} %get-tuple-element.12, f32[32]{0:T(128)S(1)} %get-tuple-element.11), channel_id=1, replica_groups=mesh['rows'=32] {'rows'}, use_global_device_ids=true, to_apply=%region_5.6 | all-reduce | flops 64 | bytes 512 | tf_op jit(solution)/shard_map/psum | solution.py:79
  183.2 6.1 %fusion.66 = f32[16,32,256]{2,1,0:T(8,128)S(1)} fusion(f32[16,256,256]{2,1,0:T(8,128)} %param.14, f32[4,16,8,256]{3,2,1,0:T(8,128)S(1)} %bitcast.219), kind=kOutput, calls=%fused_computation.57 | convolution fusion | flops 402653184 | bytes 5242880 | tf_op jit(solution)/shard_map/bij,kbj->kbi/dot_general | solution.py:75
  189.2 13.0 %fusion.74 = f32[16,32,4,256]{3,1,2,0:T(8,128)S(1)} fusion(f32[16,4,256,256]{3,2,1,0:T(8,128)} %param.10, f32[16,32,256]{2,1,0:T(8,128)S(1)} %fusion.66), kind=kOutput, calls=%fused_computation.65 | convolution fusion | flops 1610612736 | bytes 19398656 | tf_op jit(solution)/shard_map/kbi,bsij->kbsj/dot_general | solution.py:24
  202.3 2.7 collective-permute-start.4
  205.0 2.4 fusion.36
  213.4 18.8 %fusion.48 = f32[16,4,8,256]{3,2,1,0:T(8,128)S(1)} fusion(f32[16,4,256,256]{3,2,1,0:T(8,128)} %param.10, f32[32,256,16,4]{1,2,3,0:T(8,128)S(1)} %fusion.57), kind=kOutput, calls=%fused_computation.37 | convolution fusion | flops 1610612736 | bytes 19398656 | tf_op jit(solution)/shard_map/bsij,kbsj->kbi/dot_general | solution.py:28
  234.3 38.4 %all-reduce.6 = (f32[32]{0:T(128)S(1)}, f32[32]{0:T(128)S(1)}) all-reduce(f32[32]{0:T(128)S(1)} %get-tuple-element.10, f32[32]{0:T(128)S(1)} %get-tuple-element.9), channel_id=1, replica_groups=mesh['rows'=32] {'rows'}, use_global_device_ids=true, to_apply=%region_9.10 | all-reduce | flops 64 | bytes 512 | tf_op jit(solution)/shard_map/psum | solution.py:79
  273.8 6.1 %fusion.63 = f32[16,32,256]{2,1,0:T(8,128)S(1)} fusion(f32[16,256,256]{2,1,0:T(8,128)} %param.14, f32[4,16,8,256]{3,2,1,0:T(8,128)S(1)} %bitcast.224), kind=kOutput, calls=%fused_computation.54 | convolution fusion | flops 402653184 | bytes 5242880 | tf_op jit(solution)/shard_map/bij,kbj->kbi/dot_general | solution.py:75
  279.8 13.0 %fusion.72 = f32[16,32,4,256]{3,1,2,0:T(8,128)S(1)} fusion(f32[16,4,256,256]{3,2,1,0:T(8,128)} %param.10, f32[16,32,256]{2,1,0:T(8,128)S(1)} %fusion.63), kind=kOutput, calls=%fused_computation.63 | convolution fusion | flops 1610612736 | bytes 19398656 | tf_op jit(solution)/shard_map/kbi,bsij->kbsj/dot_general | solution.py:24
  302.4 3.0 fusion.55
  305.4 18.8 %fusion.51 = f32[16,4,8,256]{3,2,1,0:T(8,128)S(1)} fusion(f32[16,4,256,256]{3,2,1,0:T(8,128)} %param.10, f32[32,256,16,4]{1,2,3,0:T(8,128)S(1)} %fusion.55), kind=kOutput, calls=%fused_computation.38 | convolution fusion | flops 1610612736 | bytes 19398656 | tf_op jit(solution)/shard_map/bsij,kbsj->kbi/dot_general | solution.py:28
  325.3 41.0 %all-reduce.5 = (f32[32]{0:T(128)S(1)}, f32[32]{0:T(128)S(1)}) all-reduce(f32[32]{0:T(128)S(1)} %get-tuple-element.8, f32[32]{0:T(128)S(1)} %get-tuple-element.7), channel_id=1, replica_groups=mesh['rows'=32] {'rows'}, use_global_device_ids=true, to_apply=%region_13.14 | all-reduce | flops 64 | bytes 512 | tf_op jit(solution)/shard_map/psum | solution.py:79
  372.0 123.1 %all-reduce.11.cloned.1.call-done = (f32[96,96]{1,0:T(8,128)}, f32[96,96]{1,0:T(8,128)}) async-done(((f32[96,96]{1,0:T(8,128)}, f32[96,96]{1,0:T(8,128)}), (f32[96,96]{1,0:T(8,128)}, f32[96,96]{1,0:T(8,128)})) %all-reduce.11.cloned.1.call-update) | async-done | bytes 73744 | tf_op jit(solution)/shard_map/psum | solution.py:88
  496.9 8.8 %cholesky.20 = f32[96,96]{1,0:T(8,128)S(1)} custom-call(f32[96,96]{1,0:T(8,128)S(1)} %fusion.83), custom_call_target="Cholesky" | custom-call | tf_op jit(solution)/shard_map/jit(cholesky)/cholesky | solution.py:96
  507.0 7.4 %custom-call.8 = f32[1,96,96]{1,2,0:T(8,128)S(1)} custom-call(f32[1,96,96]{2,1,0:T(8,128)S(1)} %fusion.80), custom_call_target="InvertDiagBlocksLowerTriangular" | custom-call | tf_op jit(solution)/shard_map/jit(_solve_triangular)/triangular_solve | solution.py:98
  (119 shorter events, 45.0 us)
Async XLA Ops:
  7.2 488.0 %all-reduce.11.cloned.1.call-start = ((), (), s32[]{:S(2)}) async-start(), calls=%async_computation | async-start | bytes 196608 | tf_op jit(solution)/shard_map/psum | solution.py:88
  8.1 26.4 %collective-permute-start = (f32[32,1024]{1,0:T(8,128)S(1)}, f32[32,1024]{1,0:T(8,128)S(1)}, u32[]{:S(2)}, u32[]{:S(2)}) collective-permute-start(f32[32,1024]{1,0:T(8,128)S(1)} %slice.46), channel_id=1, source_target_pairs={{1,0},{2,1},{3,2},{4,3},{5,4},{6,5},{7,6},{8,7},{9,8},{10,9},{11,1... | collective-permute-start | bytes 393224 | tf_op jit(solution)/shard_map/ppermute | solution.py:13
  15.2 99.9 %copy-start.8 = (f32[16,4]{0,1:T(4,128)}, f32[16,4]{0,1:T(4,128)S(1)}, u32[]{:S(2)}) copy-start(f32[16,4]{0,1:T(4,128)S(1)} %fusion.125) | copy-start | bytes 772
  17.1 98.0 %copy-start.11 = (s32[16,4]{0,1:T(4,128)}, s32[16,4]{0,1:T(4,128)S(1)}, u32[]{:S(2)}) copy-start(s32[16,4]{0,1:T(4,128)S(1)} %add_select_fusion) | copy-start | bytes 772
  31.0 3.5 copy-start
  33.5 21.8 %collective-permute-start.1 = (f32[32,1024]{1,0:T(8,128)S(1)}, f32[32,1024]{1,0:T(8,128)S(1)}, u32[]{:S(2)}, u32[]{:S(2)}) collective-permute-start(f32[32,1024]{1,0:T(8,128)S(1)} %bitcast.242), channel_id=1, source_target_pairs={{31,0},{0,1},{1,2},{2,3},{3,4},{4,5},{5,6},{6,7},{7,8},{8,9},{9,10... | collective-permute-start | bytes 393224 | tf_op jit(solution)/shard_map/ppermute | solution.py:13
  36.5 18.8 %copy-start.7 = (f32[4096]{0:T(1024)S(1)}, f32[4096]{0:T(1024)}, u32[]{:S(2)}) copy-start(f32[4096]{0:T(1024)} %param.13) | copy-start | bytes 49156
  55.7 44.5 %copy-start.1 = (f32[32,4096]{1,0:T(8,128)}, f32[32,4096]{1,0:T(8,128)S(1)}, u32[]{:S(2)}) copy-start(f32[32,4096]{1,0:T(8,128)S(1)} %get-tuple-element.28) | copy-start | bytes 1572868
  94.0 6.2 %copy-start.15 = (f32[32]{0:T(128)}, f32[32]{0:T(128)S(1)}, u32[]{:S(2)}) copy-start(f32[32]{0:T(128)S(1)} %div.20) | copy-start | bytes 388
  113.3 5.9 %collective-permute-start.2 = (f32[32,1024]{1,0:T(8,128)S(1)}, f32[32,1024]{1,0:T(8,128)S(1)}, u32[]{:S(2)}, u32[]{:S(2)}) collective-permute-start(f32[32,1024]{1,0:T(8,128)S(1)} %slice.60), channel_id=1, source_target_pairs={{1,0},{2,1},{3,2},{4,3},{5,4},{6,5},{7,6},{8,7},{9,8},{10,9},{11,1... | collective-permute-start | bytes 393224 | tf_op jit(solution)/shard_map/ppermute | solution.py:13
  118.9 21.2 %collective-permute-start.3 = (f32[32,1024]{1,0:T(8,128)S(1)}, f32[32,1024]{1,0:T(8,128)S(1)}, u32[]{:S(2)}, u32[]{:S(2)}) collective-permute-start(f32[32,1024]{1,0:T(8,128)S(1)} %bitcast.243), channel_id=1, source_target_pairs={{31,0},{0,1},{1,2},{2,3},{3,4},{4,5},{5,6},{6,7},{7,8},{8,9},{9,10... | collective-permute-start | bytes 393224 | tf_op jit(solution)/shard_map/ppermute | solution.py:13
  121.2 19.5 %copy-start.4 = (f32[4,8,16,256]{3,1,2,0:T(8,128)S(1)}, f32[4,8,16,256]{3,1,2,0:T(8,128)}, u32[]{:S(2)}) copy-start(f32[4,8,16,256]{3,1,2,0:T(8,128)} %copy.64) | copy-start | bytes 1572868
  121.2 19.5 %copy-start.16 = (f32[32]{0:T(128)S(1)}, f32[32]{0:T(128)}, u32[]{:S(2)}) copy-start(f32[32]{0:T(128)} %copy-done.15) | copy-start | bytes 388
  189.2 15.7 %copy-start.10 = (f32[16,4]{0,1:T(4,128)S(1)}, f32[16,4]{0,1:T(4,128)}, u32[]{:S(2)}) copy-start(f32[16,4]{0,1:T(4,128)} %copy-done.8) | copy-start | bytes 772
  189.2 15.7 %copy-start.13 = (s32[16,4]{0,1:T(4,128)S(1)}, s32[16,4]{0,1:T(4,128)}, u32[]{:S(2)}) copy-start(s32[16,4]{0,1:T(4,128)} %copy-done.11) | copy-start | bytes 772
  202.3 7.1 %collective-permute-start.4 = (f32[32,1024]{1,0:T(8,128)S(1)}, f32[32,1024]{1,0:T(8,128)S(1)}, u32[]{:S(2)}, u32[]{:S(2)}) collective-permute-start(f32[32,1024]{1,0:T(8,128)S(1)} %slice.63), channel_id=1, source_target_pairs={{1,0},{2,1},{3,2},{4,3},{5,4},{6,5},{7,6},{8,7},{9,8},{10,9},{11,1... | collective-permute-start | bytes 393224 | tf_op jit(solution)/shard_map/ppermute | solution.py:13
  209.3 23.0 %collective-permute-start.5 = (f32[32,1024]{1,0:T(8,128)}, f32[32,1024]{1,0:T(8,128)}, u32[]{:S(2)}, u32[]{:S(2)}) collective-permute-start(f32[32,1024]{1,0:T(8,128)} %bitcast.102), channel_id=1, source_target_pairs={{31,0},{0,1},{1,2},{2,3},{3,4},{4,5},{5,6},{6,7},{7,8},{8,9},{9,10... | collective-permute-start | bytes 393224 | tf_op jit(solution)/shard_map/ppermute | solution.py:13
  213.4 18.9 %copy-start.5 = (f32[4,8,16,256]{3,1,2,0:T(8,128)S(1)}, f32[4,8,16,256]{3,1,2,0:T(8,128)}, u32[]{:S(2)}) copy-start(f32[4,8,16,256]{3,1,2,0:T(8,128)} %copy.66) | copy-start | bytes 1572868
  292.9 6.5 %collective-permute-start.6 = (f32[32,1024]{1,0:T(8,128)S(1)}, f32[32,1024]{1,0:T(8,128)S(1)}, u32[]{:S(2)}, u32[]{:S(2)}) collective-permute-start(f32[32,1024]{1,0:T(8,128)S(1)} %slice.66), channel_id=1, source_target_pairs={{1,0},{2,1},{3,2},{4,3},{5,4},{6,5},{7,6},{8,7},{9,8},{10,9},{11,1... | collective-permute-start | bytes 393224 | tf_op jit(solution)/shard_map/ppermute | solution.py:13
  299.2 25.1 %collective-permute-start.7 = (f32[32,1024]{1,0:T(8,128)}, f32[32,1024]{1,0:T(8,128)S(1)}, u32[]{:S(2)}, u32[]{:S(2)}) collective-permute-start(f32[32,1024]{1,0:T(8,128)} %bitcast.106), channel_id=1, source_target_pairs={{31,0},{0,1},{1,2},{2,3},{3,4},{4,5},{5,6},{6,7},{7,8},{8,9},{9,10... | collective-permute-start | bytes 393224 | tf_op jit(solution)/shard_map/ppermute | solution.py:13
  305.3 18.9 %copy-start.3 = (f32[4,8,16,256]{3,1,2,0:T(8,128)S(1)}, f32[4,8,16,256]{3,1,2,0:T(8,128)}, u32[]{:S(2)}) copy-start(f32[4,8,16,256]{3,1,2,0:T(8,128)} %copy.68) | copy-start | bytes 1572868
  367.9 4.1 copy-start.6
  367.9 2.0 copy-start.2
  368.0 2.0 copy-start.17
  (4 other events, 5.5 us)
Sparse Core Ops, SparseCore 0:
  372.2 122.9 all-reduce.10
where the time goes:
time: 531 us; the launch traced here: 524 us
  matrix products  170 us (32%)
  blocking collectives  159 us (30%)
  waiting for transfers between devices  123 us (23%)
  other arithmetic  29.9 us (6%)
  between operations  15.2 us (3%)
  starting transfers between devices  14.3 us (3%)
  local copies, waits for them, and re-layouts  12.8 us (2%)
    psum x1, waiting for transfers between devices, local(): lax.psum((jnp.dot(basis, basis.T, precision=lax.Precision.HIGHEST), jnp.d...  123 us
    psum x3, blocking collectives, local(): lax.psum((jnp.sum(applied * remainder, axis=1), jnp.sum(applied * applied...  120 us
    dot_general x4, matrix products, padded_apply(): jnp.einsum('bsij,kbsj->kbi', tiles, picked, precision=lax.Precision.HIGHEST)  75.2 us
    dot_general x4, matrix products, padded_apply(): jnp.einsum('kbi,bsij->kbsj', source, tiles, precision=lax.Precision.HIGHEST)  52.8 us
    psum x1, blocking collectives, local(): lax.psum((numerator_part, denominator_part), 'rows')  38.3 us
    dot_general x3, matrix products, local(): jnp.einsum('bij,kbj->kbi', precond, shaped, precision=lax.Precision.HIGHEST)  18.2 us
    ppermute x8, starting transfers between devices, shifted(): return lax.ppermute(block, axis, route)  14.2 us
  transfers between devices with their start and end apart: 9, of which 1 were waited for; matrix products, arithmetic and copies ran while one was open for 23% of the time, Pallas kernels for 0%

commit v1 on v0

v1 whole, which is shorter than its diff:
```python
import functools

import jax
import jax.numpy as jnp
from jax import lax
from jax.experimental import pallas as pl
from jax.experimental.pallas import tpu as pltpu
from jax.sharding import PartitionSpec as P

HB = 4
ITERS = 3
MESH = pl.DeviceIdType.MESH
F32 = jnp.float32
BF16 = jnp.bfloat16
NN = (((1,), (0,)), ((), ()))
NT = (((1,), (1,)), ((), ()))


def split(x):
    high = x.astype(BF16)
    low = (x - high.astype(F32)).astype(BF16)
    return high, low


def dot(a, b, dims):
    return lax.dot_general(a, b, dims, preferred_element_type=F32)


def dot3(pair, high, low, dims):
    rows = pair.shape[0] // 2
    both = dot(pair, high, dims)
    return both[:rows] + both[rows:] + dot(pair[:rows], low, dims)


def kernel(
    n, cols, counts, blocks, precond, onsite, vectors, prev_vectors, prev_image,
    correction, reduced,
    w_high, w_low, m_high, m_low, stage, pstage, field, pair, acc, image, rem, app, hcorr,
    halo_in, land_in, part, sums_in, gp, gp_in, gsum, gall, work,
    load_sem, pload_sem, halo_send, halo_recv, land_send, land_recv,
    sum_send, sum_recv, gp_send, gp_recv, ga_send, ga_recv,
):
    me = lax.axis_index("rows")
    right, left = lax.rem(me + 1, n), lax.rem(me + n - 1, n)
    br, slots, bs = blocks.shape[0], blocks.shape[1], blocks.shape[2]
    kv = vectors.shape[0]
    total = br * n
    first = br - HB

    def lanes(b):
        return pl.ds(pl.multiple_of(b * bs, bs), bs)

    def order(t):
        return lax.rem(t + first, br)

    def load(t):
        b = order(t)
        return pltpu.make_async_copy(blocks.at[b], stage.at[lax.rem(t, 3)], load_sem.at[lax.rem(t, 3)])

    def pload(b):
        return pltpu.make_async_copy(precond.at[b], pstage.at[lax.rem(b, 2)], pload_sem.at[lax.rem(b, 2)])

    load(0).start()
    load(1).start()
    load(2).start()
    pload(0).start()
    pload(1).start()

    barrier = pltpu.get_barrier_semaphore()

    def greet(d, _):
        pl.semaphore_signal(barrier, inc=1, device_id=(lax.rem(me + d, n),), device_id_type=MESH)
        return 0

    lax.fori_loop(1, n, greet, 0)

    def take_vectors(b, _):
        x = vectors[:, lanes(b)]
        field[b] = x
        high, low = split(x)
        pair[b, :kv] = high
        pair[b, kv:] = low
        return 0

    lax.fori_loop(0, br, take_vectors, 0)
    pair[br + HB] = jnp.zeros((2 * kv, bs), BF16)
    pl.semaphore_wait(barrier, n - 1)

    def offset(b, s):
        return lax.rem(cols[b, s] - (me * br + b) + total, total)

    def spread(b):
        moved = dot3(pair[b], w_high[b], w_low[b], NN)
        parts = [moved[:, s * bs:(s + 1) * bs] for s in range(slots)]
        offs = [jnp.where(s < counts[b], offset(b, s), HB + 1) for s in range(slots)]
        for k in range(HB + 1):
            got = acc[b + k]
            for s in range(slots):
                got = got + jnp.where(offs[s] == k, 1.0, 0.0).astype(F32) * parts[s]
            acc[b + k] = got

    def forward(b):
        picks = []
        for s in range(slots):
            at = jnp.where(s < counts[b], b + offset(b, s), br + HB)
            picks.append(pair[at])
        wide = jnp.concatenate(picks, axis=1)
        acc[b] = acc[b] + dot3(wide, w_high[b], w_low[b], NT)

    def take_tiles(t):
        load(t).wait()
        b = order(t)
        for s in range(slots):
            high, low = split(stage[lax.rem(t, 3), s])
            w_high[b, :, s * bs:(s + 1) * bs] = high
            w_low[b, :, s * bs:(s + 1) * bs] = low

        @pl.when(t + 3 < br)
        def _():
            load(t + 3).start()

    def operate(k, loading):
        halo = pltpu.make_async_remote_copy(
            src_ref=field.at[pl.ds(0, HB)], dst_ref=halo_in.at[k],
            send_sem=halo_send.at[k], recv_sem=halo_recv.at[k],
            device_id=(left,), device_id_type=MESH)
        halo.start()

        def clear(b, _):
            acc[b] = jnp.zeros((kv, bs), F32)
            return 0

        lax.fori_loop(0, br + HB, clear, 0)

        def late(t, _):
            if loading:
                take_tiles(t)
            spread(first + t)
            return 0

        lax.fori_loop(0, HB, late, 0)
        land = pltpu.make_async_remote_copy(
            src_ref=acc.at[pl.ds(br, HB)], dst_ref=land_in.at[k],
            send_sem=land_send.at[k], recv_sem=land_recv.at[k],
            device_id=(right,), device_id_type=MESH)
        land.start()

        def main(b, _):
            if loading:
                take_tiles(b + HB)
            spread(b)
            if not loading:
                forward(b)
            return 0

        lax.fori_loop(0, first, main, 0)
        if loading:
            def again(b, _):
                forward(b)
                return 0

            lax.fori_loop(0, first, again, 0)
        halo.wait_recv()

        def take_halo(i, _):
            high, low = split(halo_in[k, i])
            pair[br + i, :kv] = high
            pair[br + i, kv:] = low
            return 0

        lax.fori_loop(0, HB, take_halo, 0)

        def tail(b, _):
            forward(b)
            return 0

        lax.fori_loop(first, br, tail, 0)
        land.wait_recv()

        def take_land(i, _):
            acc[i] = acc[i] + land_in[k, i]
            return 0

        lax.fori_loop(0, HB, take_land, 0)
        halo.wait_send()
        land.wait_send()

    def all_sum(k, one, two):
        folded = jnp.concatenate([one, two], axis=0)
        folded = folded[:, :128] + folded[:, 128:]
        wide = jnp.broadcast_to(jnp.sum(folded, axis=1, keepdims=True), (2 * kv, 128))
        wide = jnp.concatenate([wide, jnp.zeros((128 - 2 * kv, 128), F32)], axis=0)
        mine = wide.T[:8]
        part[k] = mine
        sums_in[k, me] = mine

        def copy(d):
            return pltpu.make_async_remote_copy(
                src_ref=part.at[k], dst_ref=sums_in.at[k, me],
                send_sem=sum_send.at[k, d], recv_sem=sum_recv.at[k, me],
                device_id=(lax.rem(me + d, n),), device_id_type=MESH)

        def send(d, _):
            copy(d).start()
            return 0

        lax.fori_loop(1, n, send, 0)

        def arrive(d, _):
            who = lax.rem(me + d, n)
            pltpu.make_async_remote_copy(
                src_ref=part.at[k], dst_ref=sums_in.at[k, who],
                send_sem=sum_send.at[k, d], recv_sem=sum_recv.at[k, who],
                device_id=(who,), device_id_type=MESH).wait_recv()
            return 0

        lax.fori_loop(1, n, arrive, 0)

        def add(i, so_far):
            return so_far + sums_in[k, i]

        whole = lax.fori_loop(0, n, add, jnp.zeros((8, 128), F32))

        def sent(d, _):
            copy(d).wait_send()
            return 0

        lax.fori_loop(1, n, sent, 0)
        column = jnp.broadcast_to(whole[0:1], (128, 128)).T
        column = jnp.concatenate([column, column], axis=1)
        return column[:kv], column[kv:2 * kv]

    zero = jnp.zeros((kv, bs), F32)
    operate(0, True)

    def rayleigh(b, sums):
        x = vectors[:, lanes(b)]
        y = acc[b] + onsite[:, lanes(b)] * x
        image[b] = y
        return sums[0] + x * y, sums[1] + x * x

    numerator, denominator = all_sum(0, *lax.fori_loop(0, br, rayleigh, (zero, zero)))
    quotient = numerator / denominator

    def take_precond(b, _):
        pload(b).wait()
        high, low = split(pstage[lax.rem(b, 2)])
        m_high[b] = high
        m_low[b] = low

        @pl.when(b + 2 < br)
        def _():
            pload(b + 2).start()
        rem[b] = quotient * vectors[:, lanes(b)] - image[b]
        correction[:, lanes(b)] = zero
        hcorr[b] = zero
        return 0

    lax.fori_loop(0, br, take_precond, 0)

    for it in range(ITERS):
        def search(b, _):
            high, low = split(rem[b])
            x = dot3(jnp.concatenate([high, low], axis=0), m_high[b], m_low[b], NT)
            field[b] = x
            high, low = split(x)
            pair[b, :kv] = high
            pair[b, kv:] = low
            return 0

        lax.fori_loop(0, br, search, 0)
        operate(it + 1, False)

        def apply(b, sums):
            y = acc[b] + (onsite[:, lanes(b)] - quotient) * field[b]
            app[b] = y
            return sums[0] + y * rem[b], sums[1] + y * y

        cross, own = all_sum(it + 1, *lax.fori_loop(0, br, apply, (zero, zero)))
        step = cross / (own + 1.0)

        def update(b, _):
            x, y = field[b], app[b]
            correction[:, lanes(b)] = correction[:, lanes(b)] + step * x
            hcorr[b] = hcorr[b] + step * (y + quotient * x)
            rem[b] = rem[b] - step * y
            return 0

        lax.fori_loop(0, br, update, 0)

    nb = 3 * kv

    def gram(b, so_far):
        basis = jnp.concatenate(
            [vectors[:, lanes(b)], prev_vectors[:, lanes(b)], correction[:, lanes(b)]], axis=0)
        other = jnp.concatenate([image[b], prev_image[:, lanes(b)], hcorr[b]], axis=0)
        bh, bl = split(basis)
        oh, ol = split(other)
        high = jnp.concatenate([bh, oh], axis=0)
        low = jnp.concatenate([bl, ol], axis=0)
        return so_far + dot(bh, high, NT) + dot(bl, high, NT) + dot(bh, low, NT)

    both = lax.fori_loop(0, br, gram, jnp.zeros((nb, 2 * nb), F32))
    pad = jnp.zeros((nb, 128 - nb), F32)
    sheet = jnp.concatenate(
        [jnp.concatenate([both[:, :nb], pad], axis=1), jnp.concatenate([both[:, nb:], pad], axis=1)],
        axis=0)
    chunks = 2 * nb // 8
    for c in range(chunks):
        gp[c] = sheet[c * 8:(c + 1) * 8]

    def scatter(d):
        to = lax.rem(me + d, n)
        return to, pltpu.make_async_remote_copy(
            src_ref=gp.at[jnp.minimum(to, chunks - 1)], dst_ref=gp_in.at[me],
            send_sem=gp_send.at[d], recv_sem=gp_recv.at[me],
            device_id=(to,), device_id_type=MESH)

    def scatter_send(d, _):
        to, copy = scatter(d)

        @pl.when(to < chunks)
        def _():
            copy.start()
        return 0

    lax.fori_loop(1, n, scatter_send, 0)

    def gather(d):
        to = lax.rem(me + d, n)
        return pltpu.make_async_remote_copy(
            src_ref=gsum, dst_ref=gall.at[me],
            send_sem=ga_send.at[d], recv_sem=ga_recv.at[me],
            device_id=(to,), device_id_type=MESH)

    @pl.when(me < chunks)
    def _():
        gp_in[me] = gp[me]

        def arrive(d, _):
            who = lax.rem(me + d, n)
            pltpu.make_async_remote_copy(
                src_ref=gsum, dst_ref=gp_in.at[who],
                send_sem=gp_send.at[d], recv_sem=gp_recv.at[who],
                device_id=(who,), device_id_type=MESH).wait_recv()
            return 0

        lax.fori_loop(1, n, arrive, 0)

        def add(i, so_far):
            return so_far + gp_in[i]

        mine = lax.fori_loop(0, n, add, jnp.zeros((8, 128), F32))
        gsum[...] = mine
        gall[me] = mine

        def send(d, _):
            gather(d).start()
            return 0

        lax.fori_loop(1, n, send, 0)

    def gathered(c, _):
        @pl.when(c != me)
        def _():
            pltpu.make_async_remote_copy(
                src_ref=gsum, dst_ref=gall.at[c],
                send_sem=ga_send.at[0], recv_sem=ga_recv.at[c],
                device_id=(right,), device_id_type=MESH).wait_recv()
        return 0

    lax.fori_loop(0, chunks, gathered, 0)

    def scatter_done(d, _):
        to, copy = scatter(d)

        @pl.when(to < chunks)
        def _():
            copy.wait_send()

        @pl.when(me < chunks)
        def _():
            gather(d).wait_send()
        return 0

    lax.fori_loop(1, n, scatter_done, 0)

    rows_at = lax.broadcasted_iota(jnp.int32, (nb, 128), 0)
    cols_at = lax.broadcasted_iota(jnp.int32, (nb, 128), 1)
    eye = jnp.where(rows_at == cols_at, 1.0, 0.0).astype(F32)
    half = chunks // 2
    g = jnp.concatenate([gall[c] for c in range(half)], axis=0)
    p = jnp.concatenate([gall[half + c] for c in range(half)], axis=0)
    work[:, 0:128] = g + eye
    work[:, 128:256] = p
    work[:, 256:384] = eye

    def eliminate(j, _):
        column = jnp.sum(jnp.where(cols_at == j, work[:, 0:128], 0.0), axis=1, keepdims=True)
        row = work[pl.ds(j, 1), :]
        pivot = jnp.sum(jnp.where(lax.broadcasted_iota(jnp.int32, (1, 128), 1) == j, row[:, :128], 0.0), axis=1, keepdims=True)
        root = 1.0 / jnp.sqrt(pivot)
        row = row * root
        below = jnp.where(rows_at[:, 0:1] > j, column * root, 0.0)
        work[...] = work[...] - below * row
        work[pl.ds(j, 1), :] = row
        return 0

    lax.fori_loop(0, nb, eliminate, 0)
    half_way = work[:, 128:256]
    inverse = work[:, 256:384]
    answer = lax.dot_general(
        half_way[:, :nb], inverse[:, :nb], NT, precision=lax.Precision.HIGHEST,
        preferred_element_type=F32)
    reduced[...] = answer


def local(blocks, block_cols, live_counts, onsite_energy, precond, vectors, prev_vectors, prev_image):
    n = lax.axis_size("rows")
    br, slots, bs, _ = blocks.shape
    kv, width = vectors.shape
    nb = 3 * kv
    vmem = pl.BlockSpec(memory_space=pltpu.VMEM)
    smem = pl.BlockSpec(memory_space=pltpu.SMEM)
    hbm = pl.BlockSpec(memory_space=pl.ANY)
    dma = pltpu.SemaphoreType.DMA
    rounds = ITERS + 1
    chunks = 2 * nb // 8
    return pl.pallas_call(
        functools.partial(kernel, n),
        out_shape=(
            jax.ShapeDtypeStruct((kv, width), F32),
            jax.ShapeDtypeStruct((nb, nb), F32),
        ),
        in_specs=[smem, smem, hbm, hbm, vmem, vmem, vmem, vmem],
        out_specs=(vmem, vmem),
        scratch_shapes=[
            pltpu.VMEM((br, bs, slots * bs), BF16),
            pltpu.VMEM((br, bs, slots * bs), BF16),
            pltpu.VMEM((br, bs, bs), BF16),
            pltpu.VMEM((br, bs, bs), BF16),
            pltpu.VMEM((3, slots, bs, bs), F32),
            pltpu.VMEM((2, bs, bs), F32),
            pltpu.VMEM((br, kv, bs), F32),
            pltpu.VMEM((br + HB + 1, 2 * kv, bs), BF16),
            pltpu.VMEM((br + HB, kv, bs), F32),
            pltpu.VMEM((br, kv, bs), F32),
            pltpu.VMEM((br, kv, bs), F32),
            pltpu.VMEM((br, kv, bs), F32),
            pltpu.VMEM((br, kv, bs), F32),
            pltpu.VMEM((rounds, HB, kv, bs), F32),
            pltpu.VMEM((rounds, HB, kv, bs), F32),
            pltpu.VMEM((rounds, 8, 128), F32),
            pltpu.VMEM((rounds, n, 8, 128), F32),
            pltpu.VMEM((chunks, 8, 128), F32),
            pltpu.VMEM((n, 8, 128), F32),
            pltpu.VMEM((8, 128), F32),
            pltpu.VMEM((chunks, 8, 128), F32),
            pltpu.VMEM((nb, 384), F32),
            dma((3,)),
            dma((2,)),
            dma((rounds,)),
            dma((rounds,)),
            dma((rounds,)),
            dma((rounds,)),
            dma((rounds, n)),
            dma((rounds, n)),
            dma((n,)),
            dma((n,)),
            dma((n,)),
            dma((n,)),
        ],
        compiler_params=pltpu.CompilerParams(
            collective_id=0, has_side_effects=True, vmem_limit_bytes=60 * 1024 * 1024
        ),
    )(block_cols, live_counts, blocks, precond, onsite_energy[None, :], vectors, prev_vectors, prev_image)


def solution(mesh):
    placed = (
        P("rows", None, None, None),
        P("rows", None),
        P("rows"),
        P("rows"),
        P("rows", None, None),
        P(None, "rows"),
        P(None, "rows"),
        P(None, "rows"),
    )
    return jax.shard_map(
        local, mesh=mesh, in_specs=placed, out_specs=(P(None, "rows"), P()), check_vma=False
    )
```

time: 531 us -> 134 us (0.25); the launches traced: 524 us -> 134 us
  matrix products: 170 us -> 0 us
  blocking collectives: 159 us -> 0 us
  Pallas kernels: 0 us -> 128 us
  waiting for transfers between devices: 123 us -> 0 us
  other arithmetic: 29.9 us -> 0 us
  between operations: 15.2 us -> 0.64 us
  starting transfers between devices: 14.3 us -> 0 us
  local copies, waits for them, and re-layouts: 12.8 us -> 4.65 us
    dot_general x21 -> x0, matrix products: 168 us -> none  [the longest x4 75.2 us: padded_apply(): jnp.einsum('bsij,kbsj->kbi', tiles, picked, precision=lax.Precision.HIGHEST)]
    psum x4 -> x0, blocking collectives: 159 us -> none  [the longest x3 120 us: local(): lax.psum((jnp.sum(applied * remainder, axis=1), jnp.sum(applied * applied...]
    pallas_call x0 -> x1, Pallas kernels: none -> 128 us  [local(): pl.pallas_call(functools.partial(kernel, n), out_shape=(jax.ShapeDtypeStr...]
    psum x1 -> x0, waiting for transfers between devices: 123 us -> none  [local(): lax.psum((jnp.dot(basis, basis.T, precision=lax.Precision.HIGHEST), jnp.d...]
    another operation x5 -> x0, other arithmetic: 17.5 us -> none  [the longest x3 9.45 us: local(): factor = jnp.linalg.cholesky(gram_matrix)]
    ppermute x8 -> x0, starting transfers between devices: 14.2 us -> none  [shifted(): return lax.ppermute(block, axis, route)]
  transfers between devices with their start and end apart: 9 -> 0, of which waited for: 1 -> 0; matrix products, arithmetic and copies ran while one was open for 23% -> 0% of each run, Pallas kernels for 0% -> 0%
where the time goes in v1:
time: 134 us
  Pallas kernels  128 us (96%)
  local copies, waits for them, and re-layouts  4.65 us (3%)
    pallas_call x1, Pallas kernels, local(): pl.pallas_call(functools.partial(kernel, n), out_shape=(jax.ShapeDtypeStr...  128 us
    unnamed x3, local copies, waits for them, and re-layouts  4.65 us

profile of v1, /device:TPU:0, one launch (start us, length us, event | category | flops | bytes accessed | tf_op | source)
XLA Modules:
  0.0 133.5 jit_solution(16914917144735455968)
XLA Ops:
  0.6 1.4 %copy.10.cols = s32[16,4]{1,0:T(8,128)} copy(s32[16,4]{0,1:T(4,128)} %param.9) | data formatting | bytes 512 | tf_op args[1]
  2.0 128.2 %shard_map.95 = (f32[32,4096]{1,0:T(8,128)}, f32[96,96]{1,0:T(8,128)}) custom-call(s32[16,4]{1,0:T(8,128)} %copy.10.cols, s32[16]{0:T(128)} %counts.1, f32[16,4,256,256]{3,2,1,0:T(8,128)} %blocks.1, f32[16,256,256]{2,1,0:T(8,128)} %precond.1, f32[1,4096]{1,0:T(1,128)} %bitcast.1, f32[32,4096]{1,0:T(8,128)} %vectors.1, f32[32,4096]{1,0:T(8,128)} %prev_vectors.1, ...), custom_call_target="tpu_custom_call" | custom-call | tf_op jit(solution)/shard_map/pallas_call | solution.py:429
  130.2 1.9 %copy.13 = f32[32,4096]{1,0:T(8,128)} copy(f32[32,4096]{1,0:T(8,128)} %get-tuple-element.4) | data formatting | bytes 1048576
  132.1 1.4 %copy.14 = f32[96,96]{1,0:T(8,128)} copy(f32[96,96]{1,0:T(8,128)} %get-tuple-element.5) | data formatting | bytes 73728

commit v2 on v1

--- a/solution.py
+++ b/solution.py
@@ -35,7 +35,7 @@
 def kernel(
     n, cols, counts, blocks, precond, onsite, vectors, prev_vectors, prev_image,
     correction, reduced,
-    w_high, w_low, m_high, m_low, stage, pstage, field, pair, acc, image, rem, app, hcorr,
+    w_high, w_low, m_high, m_low, stage, pstage, field, pair, acc, image, rem, app, hcorr, srch,
     halo_in, land_in, part, sums_in, gp, gp_in, gsum, gall, work,
     load_sem, pload_sem, halo_send, halo_recv, land_send, land_recv,
     sum_send, sum_recv, gp_send, gp_recv, ga_send, ga_recv,
@@ -185,7 +185,13 @@
         halo.wait_send()
         land.wait_send()
 
-    def all_sum(k, one, two):
+    def sum_copy(k, d):
+        return pltpu.make_async_remote_copy(
+            src_ref=part.at[k], dst_ref=sums_in.at[k, me],
+            send_sem=sum_send.at[k, d], recv_sem=sum_recv.at[k, me],
+            device_id=(lax.rem(me + d, n),), device_id_type=MESH)
+
+    def sum_start(k, one, two):
         folded = jnp.concatenate([one, two], axis=0)
         folded = folded[:, :128] + folded[:, 128:]
         wide = jnp.broadcast_to(jnp.sum(folded, axis=1, keepdims=True), (2 * kv, 128))
@@ -194,18 +200,13 @@
         part[k] = mine
         sums_in[k, me] = mine
 
-        def copy(d):
-            return pltpu.make_async_remote_copy(
-                src_ref=part.at[k], dst_ref=sums_in.at[k, me],
-                send_sem=sum_send.at[k, d], recv_sem=sum_recv.at[k, me],
-                device_id=(lax.rem(me + d, n),), device_id_type=MESH)
-
         def send(d, _):
-            copy(d).start()
+            sum_copy(k, d).start()
             return 0
 
         lax.fori_loop(1, n, send, 0)
 
+    def sum_finish(k):
         def arrive(d, _):
             who = lax.rem(me + d, n)
             pltpu.make_async_remote_copy(
@@ -222,7 +223,7 @@
         whole = lax.fori_loop(0, n, add, jnp.zeros((8, 128), F32))
 
         def sent(d, _):
-            copy(d).wait_send()
+            sum_copy(k, d).wait_send()
             return 0
 
         lax.fori_loop(1, n, sent, 0)
@@ -239,8 +240,7 @@
         image[b] = y
         return sums[0] + x * y, sums[1] + x * x
 
-    numerator, denominator = all_sum(0, *lax.fori_loop(0, br, rayleigh, (zero, zero)))
-    quotient = numerator / denominator
+    sum_start(0, *lax.fori_loop(0, br, rayleigh, (zero, zero)))
 
     def take_precond(b, _):
         pload(b).wait()
@@ -251,16 +251,23 @@
         @pl.when(b + 2 < br)
         def _():
             pload(b + 2).start()
-        rem[b] = quotient * vectors[:, lanes(b)] - image[b]
         correction[:, lanes(b)] = zero
         hcorr[b] = zero
         return 0
 
     lax.fori_loop(0, br, take_precond, 0)
-
-    for it in range(ITERS):
-        def search(b, _):
-            high, low = split(rem[b])
+    numerator, denominator = sum_finish(0)
+    quotient = numerator / denominator
+
+    def begin(b, _):
+        rem[b] = quotient * vectors[:, lanes(b)] - image[b]
+        return 0
+
+    lax.fori_loop(0, br, begin, 0)
+
+    def precondition(source):
+        def body(b, _):
+            high, low = split(source[b])
             x = dot3(jnp.concatenate([high, low], axis=0), m_high[b], m_low[b], NT)
             field[b] = x
             high, low = split(x)
@@ -268,25 +275,44 @@
             pair[b, kv:] = low
             return 0
 
-        lax.fori_loop(0, br, search, 0)
-        operate(it + 1, False)
-
-        def apply(b, sums):
-            y = acc[b] + (onsite[:, lanes(b)] - quotient) * field[b]
-            app[b] = y
-            return sums[0] + y * rem[b], sums[1] + y * y
-
-        cross, own = all_sum(it + 1, *lax.fori_loop(0, br, apply, (zero, zero)))
+        lax.fori_loop(0, br, body, 0)
+
+    precondition(rem)
+    operate(1, False)
+
+    def apply(b, sums):
+        x = field[b]
+        y = acc[b] + (onsite[:, lanes(b)] - quotient) * x
+        srch[b] = x
+        app[b] = y
+        return sums[0] + y * rem[b], sums[1] + y * y
+
+    sum_start(1, *lax.fori_loop(0, br, apply, (zero, zero)))
+    for it in range(ITERS):
+        last = it == ITERS - 1
+        if not last:
+            precondition(app)
+            operate(it + 2, False)
+        cross, own = sum_finish(it + 1)
         step = cross / (own + 1.0)
 
-        def update(b, _):
-            x, y = field[b], app[b]
+        def update(b, sums):
+            x, y = srch[b], app[b]
             correction[:, lanes(b)] = correction[:, lanes(b)] + step * x
             hcorr[b] = hcorr[b] + step * (y + quotient * x)
-            rem[b] = rem[b] - step * y
-            return 0
-
-        lax.fori_loop(0, br, update, 0)
+            if last:
+                return sums
+            turned = field[b]
+            r = rem[b] - step * y
+            z = y - step * (acc[b] + (onsite[:, lanes(b)] - quotient) * turned)
+            srch[b] = x - step * turned
+            rem[b] = r
+            app[b] = z
+            return sums[0] + z * r, sums[1] + z * z
+
+        sums = lax.fori_loop(0, br, update, (zero, zero))
+        if not last:
+            sum_start(it + 2, *sums)
 
     nb = 3 * kv
 
@@ -448,6 +474,7 @@
             pltpu.VMEM((br, kv, bs), F32),
             pltpu.VMEM((br, kv, bs), F32),
             pltpu.VMEM((br, kv, bs), F32),
+            pltpu.VMEM((br, kv, bs), F32),
             pltpu.VMEM((rounds, HB, kv, bs), F32),
             pltpu.VMEM((rounds, HB, kv, bs), F32),
             pltpu.VMEM((rounds, 8, 128), F32),

time: 134 us -> 118 us (0.88)
  Pallas kernels: 128 us -> 113 us
    pallas_call x1, Pallas kernels: 128 us -> 113 us  [local(): pl.pallas_call(functools.partial(kernel, n), out_shape=(jax.ShapeDtypeStr...]
where the time goes in v2:
time: 118 us
  Pallas kernels  113 us (96%)
  local copies, waits for them, and re-layouts  4.65 us (4%)
    pallas_call x1, Pallas kernels, local(): pl.pallas_call(functools.partial(kernel, n), out_shape=(jax.ShapeDtypeStr...  113 us
    unnamed x3, local copies, waits for them, and re-layouts  4.65 us

profile of v2, /device:TPU:0, one launch (start us, length us, event | category | flops | bytes accessed | tf_op | source)
XLA Modules:
  0.0 117.9 jit_solution(16123429101809145066)
XLA Ops:
  0.6 1.4 %copy.10.cols = s32[16,4]{1,0:T(8,128)} copy(s32[16,4]{0,1:T(4,128)} %param.9) | data formatting | bytes 512 | tf_op args[1]
  2.0 112.6 %shard_map.95 = (f32[32,4096]{1,0:T(8,128)}, f32[96,96]{1,0:T(8,128)}) custom-call(s32[16,4]{1,0:T(8,128)} %copy.10.cols, s32[16]{0:T(128)} %counts.1, f32[16,4,256,256]{3,2,1,0:T(8,128)} %blocks.1, f32[16,256,256]{2,1,0:T(8,128)} %precond.1, f32[1,4096]{1,0:T(1,128)} %bitcast.1, f32[32,4096]{1,0:T(8,128)} %vectors.1, f32[32,4096]{1,0:T(8,128)} %prev_vectors.1, ...), custom_call_target="tpu_custom_call" | custom-call | tf_op jit(solution)/shard_map/pallas_call | solution.py:455
  114.6 1.9 %copy.13 = f32[32,4096]{1,0:T(8,128)} copy(f32[32,4096]{1,0:T(8,128)} %get-tuple-element.4) | data formatting | bytes 1048576
  116.5 1.4 %copy.14 = f32[96,96]{1,0:T(8,128)} copy(f32[96,96]{1,0:T(8,128)} %get-tuple-element.5) | data formatting | bytes 73728

commit v3 on v2

--- a/solution.py
+++ b/solution.py
@@ -138,7 +138,7 @@
             spread(first + t)
             return 0
 
-        lax.fori_loop(0, HB, late, 0)
+        lax.fori_loop(0, HB, late, 0, unroll=1 if loading else 2)
         land = pltpu.make_async_remote_copy(
             src_ref=acc.at[pl.ds(br, HB)], dst_ref=land_in.at[k],
             send_sem=land_send.at[k], recv_sem=land_recv.at[k],
@@ -153,13 +153,13 @@
                 forward(b)
             return 0
 
-        lax.fori_loop(0, first, main, 0)
+        lax.fori_loop(0, first, main, 0, unroll=1 if loading else 2)
         if loading:
             def again(b, _):
                 forward(b)
                 return 0
 
-            lax.fori_loop(0, first, again, 0)
+            lax.fori_loop(0, first, again, 0, unroll=2)
         halo.wait_recv()
 
         def take_halo(i, _):
@@ -174,7 +174,7 @@
             forward(b)
             return 0
 
-        lax.fori_loop(first, br, tail, 0)
+        lax.fori_loop(first, br, tail, 0, unroll=2)
         land.wait_recv()
 
         def take_land(i, _):
@@ -275,7 +275,7 @@
             pair[b, kv:] = low
             return 0
 
-        lax.fori_loop(0, br, body, 0)
+        lax.fori_loop(0, br, body, 0, unroll=4)
 
     precondition(rem)
     operate(1, False)
@@ -310,7 +310,7 @@
             app[b] = z
             return sums[0] + z * r, sums[1] + z * z
 
-        sums = lax.fori_loop(0, br, update, (zero, zero))
+        sums = lax.fori_loop(0, br, update, (zero, zero), unroll=2)
         if not last:
             sum_start(it + 2, *sums)
 
@@ -326,7 +326,7 @@
         low = jnp.concatenate([bl, ol], axis=0)
         return so_far + dot(bh, high, NT) + dot(bl, high, NT) + dot(bh, low, NT)
 
-    both = lax.fori_loop(0, br, gram, jnp.zeros((nb, 2 * nb), F32))
+    both = lax.fori_loop(0, br, gram, jnp.zeros((nb, 2 * nb), F32), unroll=2)
     pad = jnp.zeros((nb, 128 - nb), F32)
     sheet = jnp.concatenate(
         [jnp.concatenate([both[:, :nb], pad], axis=1), jnp.concatenate([both[:, nb:], pad], axis=1)],
@@ -424,17 +424,17 @@
     def eliminate(j, _):
         column = jnp.sum(jnp.where(cols_at == j, work[:, 0:128], 0.0), axis=1, keepdims=True)
         row = work[pl.ds(j, 1), :]
-        pivot = jnp.sum(jnp.where(lax.broadcasted_iota(jnp.int32, (1, 128), 1) == j, row[:, :128], 0.0), axis=1, keepdims=True)
-        root = 1.0 / jnp.sqrt(pivot)
-        row = row * root
-        below = jnp.where(rows_at[:, 0:1] > j, column * root, 0.0)
+        pivot = jnp.sum(jnp.where(lane_at == j, row[:, :128], 0.0), axis=1, keepdims=True)
+        below = jnp.where(rows_at[:, 0:1] > j, column / pivot, 0.0)
         work[...] = work[...] - below * row
-        work[pl.ds(j, 1), :] = row
-        return 0
-
-    lax.fori_loop(0, nb, eliminate, 0)
-    half_way = work[:, 128:256]
-    inverse = work[:, 256:384]
+        return 0
+
+    lane_at = lax.broadcasted_iota(jnp.int32, (1, 128), 1)
+    lax.fori_loop(0, nb, eliminate, 0, unroll=2)
+    diagonal = jnp.sum(jnp.where(rows_at == cols_at, work[:, 0:128], 0.0), axis=1, keepdims=True)
+    scale = 1.0 / jnp.sqrt(diagonal)
+    half_way = scale * work[:, 128:256]
+    inverse = scale * work[:, 256:384]
     answer = lax.dot_general(
         half_way[:, :nb], inverse[:, :nb], NT, precision=lax.Precision.HIGHEST,
         preferred_element_type=F32)

time: 118 us -> 107 us (0.907)
  Pallas kernels: 113 us -> 101 us
    pallas_call x1, Pallas kernels: 113 us -> 101 us  [local(): pl.pallas_call(functools.partial(kernel, n), out_shape=(jax.ShapeDtypeStr...]
where the time goes in v3:
time: 107 us; the launch traced here: 106 us
  Pallas kernels  101 us (94%)
  local copies, waits for them, and re-layouts  4.65 us (4%)
    pallas_call x1, Pallas kernels, local(): pl.pallas_call(functools.partial(kernel, n), out_shape=(jax.ShapeDtypeStr...  101 us
    unnamed x3, local copies, waits for them, and re-layouts  4.65 us

profile of v3, /device:TPU:0, one launch (start us, length us, event | category | flops | bytes accessed | tf_op | source)
XLA Modules:
  0.0 106.0 jit_solution(8896023498955975744)
XLA Ops:
  0.6 1.4 %copy.10.cols = s32[16,4]{1,0:T(8,128)} copy(s32[16,4]{0,1:T(4,128)} %param.9) | data formatting | bytes 512 | tf_op args[1]
  2.0 100.7 %shard_map.95 = (f32[32,4096]{1,0:T(8,128)}, f32[96,96]{1,0:T(8,128)}) custom-call(s32[16,4]{1,0:T(8,128)} %copy.10.cols, s32[16]{0:T(128)} %counts.1, f32[16,4,256,256]{3,2,1,0:T(8,128)} %blocks.1, f32[16,256,256]{2,1,0:T(8,128)} %precond.1, f32[1,4096]{1,0:T(1,128)} %bitcast.1, f32[32,4096]{1,0:T(8,128)} %vectors.1, f32[32,4096]{1,0:T(8,128)} %prev_vectors.1, ...), custom_call_target="tpu_custom_call" | custom-call | tf_op jit(solution)/shard_map/pallas_call | solution.py:455
  102.7 1.9 %copy.13 = f32[32,4096]{1,0:T(8,128)} copy(f32[32,4096]{1,0:T(8,128)} %get-tuple-element.4) | data formatting | bytes 1048576
  104.6 1.4 %copy.14 = f32[96,96]{1,0:T(8,128)} copy(f32[96,96]{1,0:T(8,128)} %get-tuple-element.5) | data formatting | bytes 73728
